TPU v7x, 32 devices: a whole 2x2x4 slice. The times are simulated.
32 devices in a mesh: band: 4 (over x, core), grid: 8 (over z, y).
Axes of the slice: x: 2, y: 2, z: 4, core: 2. Of those that a mesh axis runs over, the one named last changes fastest.
Arguments:
- orbitals: float32 [8, 128, 128, 128], P('band', 'grid'), may hold values from -6 to 6
- occupation: float32 [8], P('band'), may hold values from 0.25 to 1
- g_list: int32 [131072], P('grid'), may hold values from 0 to 262143, as said below
- positions: float32 [3, 512], replicated, may hold values from 0 to 1
- species: int32 [512], replicated, may hold values from 0 to 3
- widths: float32 [4], replicated, may hold values from 0.3 to 2
Outputs:
- stress: float32 [3, 3], replicated
- atom_terms: float32 [512], replicated
Inputs may be any that keep to these rules, and one draw needn't show every extreme that they name: `g_list`: within each aligned block of 16384 entries the values are distinct and increasing.
All inputs are finite; a program needn't handle non-finite values.
Results may differ from a plain program's by a relative error of at most 0.00013.
Values sent between devices are 32-bit elements; how exact they have to be, the bound alone decides.
A program may use at most 64 MiB of HBM per device.

v0:
```python
import functools
import math

import jax
import jax.numpy as jnp
import numpy as np
from jax import lax
from jax.experimental import pallas as pl
from jax.experimental.pallas import tpu as pltpu
from jax.sharding import PartitionSpec as P

HIGHEST = lax.Precision.HIGHEST
MESH = pl.DeviceIdType.MESH
TWO_PI = 2.0 * math.pi
F32 = jnp.float32
BF16 = jnp.bfloat16
LANES = 128
DEPTH = 8
HOP_LAG = 4
CUTS = 4
VMEM_LIMIT = 63 * 1024 * 1024

BATCHES = (
    ((0, 0, 1.0), (0, 1, 2.0), (1, 1, 1.0), (0, 2, 2.0), (1, 3, 2.0)),
    ((0, 4, 2.0), (0, 5, 2.0), (1, 4, 2.0), (1, 5, 2.0)),
)


def trig(rows, columns, length):
    angles = TWO_PI / length * (rows[:, None] * columns[None, :] % length)
    return np.cos(angles), np.sin(angles)


def halves(table):
    table = np.asarray(table, np.float32)
    high = table.astype(jnp.bfloat16)
    low = (table - high.astype(np.float32)).astype(jnp.bfloat16)
    return high, low


def split(value):
    high = value.astype(BF16)
    low = (value - high.astype(F32)).astype(BF16)
    return high, low


def dot(a, b):
    return jnp.dot(a, b, preferred_element_type=F32)


def constant_tables(slab_x, grids, size_y, size_z):
    size_x = slab_x * grids
    half = slab_x // 2
    depth = DEPTH
    assert half <= depth
    quarter = size_y // 4
    rows = -(-(quarter + 1) // 8) * 8
    cells = float(size_x) * size_y * size_z
    bases = []
    for core in range(2):
        cosine, sine = trig(quarter * core + np.arange(quarter + 1), np.arange(size_y), size_y)
        stack = np.zeros((2, rows, size_y))
        stack[0, : quarter + 1], stack[1, : quarter + 1] = cosine / cells, sine / cells
        bases.append(stack.reshape(2 * rows, size_y))
    high, low = halves(np.stack(bases))
    basis_wide = np.concatenate([high, high], axis=2)
    cosine, sine = trig(np.arange(size_z), np.arange(size_z), size_z)
    z_high, z_low = halves(np.concatenate([cosine, sine], axis=1))
    table_wide = np.concatenate([z_high, z_high], axis=0)
    odd = 2 * np.arange(depth) + 1
    cosine, sine = trig(odd, np.arange(size_x), 2 * size_x)
    turns = np.zeros((grids, 2 * depth + 8, size_x))
    turns[:, :depth], turns[:, depth : 2 * depth] = cosine, sine
    centre = 2 * slab_x * np.arange(grids) + slab_x - 1
    turns[:, 2 * depth], turns[:, 2 * depth + 1] = trig(centre, np.arange(size_x), 2 * size_x)
    return basis_wide, low, table_wide, z_low, turns.astype(np.float32)


def cosine_of_turns(turns):
    nodes = 0.25 * np.cos((np.arange(400) + 0.5) * np.pi / 400)
    powers = nodes[:, None] ** (2 * np.arange(6)[None, :])
    fit = np.linalg.lstsq(powers, np.sin(TWO_PI * nodes) / nodes, rcond=None)[0]
    u = 0.25 - jnp.abs(turns)
    square = u * u
    value = jnp.full_like(square, float(fit[5]))
    for c in fit[4::-1]:
        value = value * square + float(c)
    return u * value


def pad_kernel(planes, items, ends, at, codes, out):
    out[...] = jnp.full_like(out, -1)
    lane = lax.broadcasted_iota(jnp.int32, (1, LANES), 1)
    flat = lax.broadcasted_iota(jnp.int32, (8, LANES), 0) * LANES + lax.broadcasted_iota(jnp.int32, (8, LANES), 1)

    def one_plane(k, carry):
        start = jnp.where(k == 0, 0, ends[jnp.maximum(k - 1, 0)])
        end = ends[k]
        count = lax.div(end - start + LANES - 1, LANES)

        def one_row(c, carry):
            place, marks = carry
            source = start + c * LANES
            row, shift = lax.div(source, LANES), lax.rem(source, LANES)
            index = jnp.broadcast_to(lax.rem(lane + shift, LANES), (8, LANES))
            pick = lambda r: jnp.take_along_axis(
                jnp.broadcast_to(codes[pl.ds(r, 1), :], (8, LANES)), index, axis=1
            )[0:1]
            value = jnp.where(lane + shift < LANES, pick(row), pick(row + 1))
            out[pl.ds(place, 1), :] = jnp.where(source + lane < end, value, -1)
            return place + 1, jnp.where(flat == place, at[0] + at[1] * k, marks)

        return lax.fori_loop(0, count, one_row, carry)

    marks = lax.fori_loop(0, planes, one_plane, (0, jnp.zeros((8, LANES), jnp.int32)))[1]
    out[pl.ds(items, 8), :] = marks


def pad_planes(codes, ends, at, items):
    return pl.pallas_call(
        functools.partial(pad_kernel, ends.shape[0], items),
        out_shape=jax.ShapeDtypeStruct((items + 8, LANES), jnp.int32),
        grid_spec=pltpu.PrefetchScalarGridSpec(
            num_scalar_prefetch=2,
            grid=(1,),
            in_specs=[pl.BlockSpec(codes.shape, lambda i, *_: (0, 0))],
            out_specs=pl.BlockSpec((items + 8, LANES), lambda i, *_: (0, 0)),
        ),
        name="pad_planes",
    )(ends, at, codes)


def exchange_kernel(
    plan,
    own, listing, atoms, basis_wide, basis_low, table_wide, table_low, turns, out,
    store, planes_a, planes_b, part_a, part_b, box_a, box_b, lists, marks, power, heard, votes, waves, sums,
    list_send, list_recv, mark_sem, side_send, side_recv, mate_send, mate_recv, lane_send, lane_recv,
    far_send, far_recv, hand_send, hand_recv, away_send, away_recv, pass_send, pass_recv, copy_sem,
    hop_send, hop_recv, share_send, share_recv, vote_send, vote_recv,
):
    size_x, slabs, items, pieces, share, kept = plan
    band, grid = lax.axis_index("band"), lax.axis_index("grid")
    bands, grids = lax.axis_size("band"), lax.axis_size("grid")
    core, x = lax.rem(band, 2), lax.div(band, 2)
    mate, link = lax.rem(grid, 2), lax.div(grid, 2)
    links = grids // 2
    everyone = bands * grids
    me = band * grids + grid
    slab_x, size_y, size_z = own.shape[1:]
    planes, parts, boxes = (planes_a, planes_b), (part_a, part_b), (box_a, box_b)
    leads = core == mate
    quarter = grids // 4
    height = items + 8
    rows = basis_low.shape[0] // 2
    kept_rows = size_y // 4 + 1

    def at(index):
        return {"band": lax.div(index, grids), "grid": lax.rem(index, grids)}

    barrier = pltpu.get_barrier_semaphore()

    def greet(step, carry):
        pl.semaphore_signal(barrier, inc=1, device_id=at(lax.rem(me + step, everyone)), device_id_type=MESH)
        return carry

    lax.fori_loop(1, everyone, greet, 0)
    pl.semaphore_wait(barrier, everyone - 1)

    def remote(source, target, send, recv, device):
        return pltpu.make_async_remote_copy(
            src_ref=source, dst_ref=target, send_sem=send, recv_sem=recv,
            device_id=device, device_id_type=MESH,
        )

    beside = {"band": band + 1 - 2 * core}
    across = {"grid": grid + 1 - 2 * mate}
    far = {"band": lax.rem(band + bands // 2, bands)}

    slot_of = lambda g, c: lax.rem(g + grids - jnp.where(c == 1, quarter, 3 * quarter), grids)
    middle = jnp.logical_and(grid >= quarter, grid < 3 * quarter)
    lists_here = middle == (core == 1)
    my_slot = slot_of(grid, core)

    def list_copy(slot, step):
        return remote(
            listing, lists.at[pl.ds(pl.multiple_of(slot * height, 8), height)],
            list_send.at[step - 1], list_recv.at[slot], {"grid": lax.rem(grid + step, grids)},
        )

    own_list = pltpu.make_async_copy(
        listing, lists.at[pl.ds(pl.multiple_of(my_slot * height, 8), height)], copy_sem.at[1]
    )

    @pl.when(lists_here)
    def _():
        def send(step, carry):
            list_copy(my_slot, step).start()
            return carry

        lax.fori_loop(1, grids, send, 0)
        own_list.start()

    cut = slab_x // (CUTS // 2)
    place = lambda group, slab, c: store.at[(group * 2 + slab) * 2 + c % 2, pl.ds(c // 2 * cut, cut)]
    mine = lambda c: own.at[c % 2, pl.ds(c // 2 * cut, cut)]
    to_side = lambda c: remote(mine(c), place(1, 0, c), side_send.at[c], side_recv.at[c], beside)
    to_mate = lambda c: remote(mine(c), place(0, 1, c), mate_send.at[c], mate_recv.at[c], across)
    to_far = lambda c: remote(mine(c), place(2, 0, c), far_send.at[c], far_recv.at[c], far)
    hand_on = lambda c: remote(place(2, 0, c), place(2, 0, c), hand_send.at[c], hand_recv.at[c], beside)
    mate_side = lambda c: remote(place(0, 1, c), place(1, 1, c), lane_send.at[c], lane_recv.at[c], beside)
    mate_far = lambda c: remote(place(0, 1, c), place(2, 1, c), away_send.at[c], away_recv.at[c], far)
    mate_hand = lambda c: remote(place(2, 1, c), place(2, 1, c), pass_send.at[c], pass_recv.at[c], beside)
    keep = pltpu.make_async_copy(own, store.at[pl.ds(0, 2)], copy_sem.at[0])
    keep.start()
    for c in range(CUTS):
        to_side(c).start()
        to_mate(c).start()

    @pl.when(leads)
    def _():
        for c in range(CUTS):
            to_far(c).start()

    def relay_far(c):
        @pl.when(leads)
        def _():
            to_far(c).wait_recv()
            hand_on(c).start()

    def relay_mate(c):
        to_mate(c).wait_recv()
        mate_side(c).start()

        @pl.when(leads)
        def _():
            mate_far(c).start()

    def relay_mate_far(c):
        @pl.when(leads)
        def _():
            mate_far(c).wait_recv()
            mate_hand(c).start()

    main = jnp.where(core == lax.rem(x + mate, 2), 0, 1)
    other = 1 - main
    base_of = (
        main * 4, main * 4 + 1, other * 4 + mate, other * 4 + 1 - mate, 8, 9,
    )

    def transform(batch, slab):
        pairs, target = BATCHES[batch], planes[batch]
        width = len(pairs) * 4 * DEPTH
        half = slab_x // 2
        unroll = math.gcd(half, 4)
        pick = lambda which, p: sum(
            jnp.where(p == q, base_of[pair[which]], 0) for q, pair in enumerate(pairs)
        ) + 2 * slab
        if half < DEPTH and slab == 0:
            target[...] = jnp.zeros_like(target)

        flat = target.reshape(kept_rows * width, size_z)

        def one_pair(p, carry):
            left, right = pick(0, p), pick(1, p)
            for block in range(half // unroll):
                stack = []
                for u in range(unroll):
                    up = half + block * unroll + u
                    down = half - 1 - block * unroll - u
                    above = store[left, up] * store[right, up]
                    below = store[left, down] * store[right, down]
                    stack += [above + below, above - below]
                high, low = split(jnp.concatenate(stack, axis=1))
                along = dot(basis_wide[...], jnp.concatenate([high, low], axis=0))
                along = along + dot(basis_low[...], high)
                stack = [along[:, i * size_z : (i + 1) * size_z] for i in range(2 * unroll)]
                high, low = split(jnp.concatenate(stack, axis=0))
                both = dot(jnp.concatenate([high, low], axis=1), table_wide[...])
                both = both + dot(high, table_low[...])
                for u in range(unroll):
                    for sign in range(2):
                        begin = (2 * u + sign) * 2 * rows
                        cosine, sine = both[begin : begin + rows], both[begin + rows : begin + 2 * rows]
                        real = cosine[:, :size_z] - sine[:, size_z:]
                        imag = -(cosine[:, size_z:] + sine[:, :size_z])
                        for part, value in ((0, real), (1, imag)):
                            row = (p * 4 + 2 * sign + part) * DEPTH + block * unroll + u
                            flat[pl.ds(row, kept_rows, stride=width), :] = value[:kept_rows]
            return carry

        lax.fori_loop(0, len(pairs), one_pair, 0)

    def code_row(t):
        slot, r = lax.div(t, items), lax.rem(t, items)
        return slot, r, lists[pl.ds(slot * height + r, 1), :]

    def select(batch, slab, group):
        pairs, source, part = BATCHES[batch], planes[batch], parts[batch]
        count = len(pairs)
        for u in range(4):
            slot, r, code = code_row(group * 4 + u)
            k = marks[slot * 8 + lax.div(r, LANES), lax.rem(r, LANES)]
            x_of = jnp.broadcast_to(lax.shift_right_arithmetic(code, size_z.bit_length() - 1) & (size_x - 1), (8, LANES))
            z_of = jnp.broadcast_to(code & (size_z - 1), (8, LANES))
            turn = lambda i: jnp.take_along_axis(turns[slab, pl.ds(8 * i, 8), :], x_of, axis=1)
            cosine, sine, phase = turn(0), turn(1), turn(2)
            phase_cos, phase_sin = phase[0:1], phase[1:2]
            for p in range(count):
                get = lambda i: jnp.take_along_axis(source[k, pl.ds((p * 4 + i) * 8, 8), :], z_of, axis=1)
                real = jnp.sum(get(0) * cosine + get(3) * sine, axis=0, keepdims=True)
                imag = jnp.sum(get(1) * cosine - get(2) * sine, axis=0, keepdims=True)
                for which, value in (
                    (0, real * phase_cos + imag * phase_sin),
                    (4, imag * phase_cos - real * phase_sin),
                ):
                    row = pl.ds(group * (8 * count) + p * 8 + which + u, 1)
                    part[row, :] = value if slab == 0 else part[row, :] + value

    groups = slabs * items // 4
    half_groups = groups // 2
    piece = half_groups // pieces

    begins = lambda upward: link == (0 if upward else links - 1)
    ends = lambda upward: link == (links - 1 if upward else 0)

    def hop(batch, upward, j, source):
        tall = piece * 8 * len(BATCHES[batch])
        rows_at = pl.ds(pl.multiple_of((j + (pieces if upward else 0)) * tall, 8), tall)
        sem = ((batch * 2 + (0 if upward else 1)) * pieces) + j
        step = 2 if upward else grids - 2
        return rows_at, remote(
            source.at[rows_at], boxes[batch].at[rows_at], hop_send.at[sem], hop_recv.at[sem],
            {"grid": lax.rem(grid + step, grids)},
        )

    def forward(batch, upward, j):
        at_rows, copy = hop(batch, upward, j, boxes[batch])
        copy.wait_recv()
        box, part = boxes[batch], parts[batch]
        box[at_rows] = box[at_rows] + part[at_rows]

        @pl.when(jnp.logical_not(ends(upward)))
        def _():
            copy.start()

        @pl.when(ends(upward))
        def _():
            value = box[at_rows].reshape(piece, len(BATCHES[batch]), 8, LANES)
            total = 0.0
            for p, pair in enumerate(BATCHES[batch]):
                total = total + pair[2] * value[:, p] * value[:, p]
            total = total.reshape(piece * 8, LANES)
            spot = pl.ds(pl.multiple_of(j * (piece * 8), 8), piece * 8)
            power[spot] = total if batch == 0 else power[spot] + total

    def chain_step(step):
        for upward in (True, False):
            hops = link if upward else links - 1 - link
            j = step - HOP_LAG * hops
            for batch in range(2):
                inside = jnp.logical_and(j >= batch * pieces, j < (batch + 1) * pieces)

                @pl.when(jnp.logical_and(inside, hops > 0))
                def _():
                    forward(batch, upward, j - batch * pieces)

    def wave_parts(t):
        slot, r, code = code_row(t)
        k = marks[slot * 8 + lax.div(r, LANES), lax.rem(r, LANES)]
        valid = code >= 0
        x_of = lax.shift_right_arithmetic(code, size_z.bit_length() - 1) & (size_x - 1)
        z_of = code & (size_z - 1)
        upper = jnp.where((slot >= quarter) == (core == 1), 1, 0)
        fold = lambda cell, size: jnp.where(cell < size // 2 + upper, cell, cell - size).astype(F32)
        kx, kz = fold(x_of, size_x), fold(z_of, size_z)
        ky = jnp.broadcast_to(k + core * (size_y // 4), (1, LANES)).astype(F32)
        gx, gy, gz = TWO_PI / size_x * kx, TWO_PI / size_y * ky, TWO_PI / size_z * kz
        square = gx * gx + gy * gy + gz * gz
        nonzero = jnp.where(square > 0, 1.0, 0.0)
        inverse = nonzero / (square + 1.0 - nonzero)
        inverse = jnp.where(valid, inverse, 0.0)
        return kx, ky, kz, gx, gy, gz, square, inverse

    count_atoms = atoms.shape[1]
    stride = 64

    def wave_block(values, b):
        kx, ky, kz = values[:3]
        at_atoms = pl.ds(b * stride, stride)
        turn = kx * atoms[0, at_atoms] + ky * atoms[1, at_atoms] + kz * atoms[2, at_atoms]
        turn = turn - jnp.floor(turn + 0.5)
        return jnp.exp(values[6] * atoms[3, at_atoms]) * cosine_of_turns(turn)

    near = 2 * (bands // 2) * links // 2
    my_class = x * 2 + mate
    offset = jnp.where(link < links // 2, 0, near)
    order = link * (2 * (bands // 2)) + my_class
    first_chunk = order * share

    for c in range(CUTS):
        to_side(c).wait_recv()
    keep.wait()
    transform(0, 0)

    for slot in range(slabs):
        from_here = jnp.logical_and(lists_here, my_slot == slot)

        @pl.when(jnp.logical_not(from_here))
        def _():
            list_copy(slot, 1).wait_recv()

        @pl.when(from_here)
        def _():
            own_list.wait()

    def mark_copy(slot):
        return pltpu.make_async_copy(
            lists.at[pl.ds(pl.multiple_of(slot * height + items, 8), 8)],
            marks.at[pl.ds(pl.multiple_of(slot * 8, 8), 8)], mark_sem.at[slot],
        )

    for slot in range(slabs):
        mark_copy(slot).start()
    for slot in range(slabs):
        mark_copy(slot).wait()

    def select_run(batch, slab, low, high):
        def body(group, carry):
            select(batch, slab, group)
            return carry

        lax.fori_loop(low, high, body, 0)

    spans = [groups * i // CUTS for i in range(CUTS + 1)]
    for c in range(CUTS):
        relay_far(c)
        select_run(0, 0, spans[c], spans[c + 1])
        if c < CUTS // 2:
            relay_mate(c)

    @pl.when(jnp.logical_not(leads))
    def _():
        for c in range(CUTS):
            hand_on(c).wait_recv()

    transform(1, 0)
    for c in range(CUTS):
        if c < CUTS // 2:
            relay_mate(c + CUTS // 2)
        relay_mate_far(c)
        select_run(1, 0, spans[c], spans[c + 1])

    for c in range(CUTS):
        mate_side(c).wait_recv()
    transform(0, 1)

    def one_piece(batch):
        def body(i, carry):
            for upward in (True, False):
                base = (i + (pieces if upward else 0)) * piece
                select_run(batch, 1, base, base + piece)

                @pl.when(begins(upward))
                def _():
                    hop(batch, upward, i, parts[batch])[1].start()

            chain_step(i + batch * pieces)
            return carry

        return body

    lax.fori_loop(0, pieces, one_piece(0), 0)

    @pl.when(jnp.logical_not(leads))
    def _():
        for c in range(CUTS):
            mate_hand(c).wait_recv()

    transform(1, 1)
    lax.fori_loop(0, pieces, one_piece(1), 0)

    def keep_wave(q, carry):
        values = wave_parts(first_chunk + q)
        for b in range(count_atoms // stride):
            waves[q, pl.ds(b * stride, stride)] = wave_block(values, b)
        return carry

    def run_out(step, carry):
        chain_step(step)
        return carry

    last = 2 * pieces
    lax.fori_loop(0, kept, keep_wave, 0)
    lax.fori_loop(last, last + HOP_LAG * (links - 1), run_out, 0)

    owner = jnp.logical_or(link == 0, link == links - 1)

    def member(index):
        at_link, at_class = lax.div(index, 2 * (bands // 2)), lax.rem(index, 2 * (bands // 2))
        return {"band": lax.div(at_class, 2) * 2 + core, "grid": at_link * 2 + lax.rem(at_class, 2)}

    tall = share * 2

    def deliver(index):
        return remote(
            power.at[pl.ds(pl.multiple_of(index * tall, 8), tall)], heard.at[my_class],
            share_send.at[index], share_recv.at[my_class], member(index + offset),
        )

    @pl.when(owner)
    def _():
        def send(index, carry):
            @pl.when(index + offset != order)
            def _():
                deliver(index).start()
            return carry

        lax.fori_loop(0, near, send, 0)
        heard[my_class] = power[pl.ds(pl.multiple_of((order - offset) * tall, 8), tall)]

    for sender in range(2 * (bands // 2)):
        @pl.when(jnp.logical_not(jnp.logical_and(owner, my_class == sender)))
        def _():
            remote(
                power.at[pl.ds(0, tall)], heard.at[sender], share_send.at[0], share_recv.at[sender],
                {"grid": lax.rem(grid + 2, grids)},
            ).wait_recv()

    total = heard[0]
    for sender in range(1, 2 * (bands // 2)):
        total = total + heard[sender]
    heard[0] = total

    zero = jnp.zeros((1, LANES), F32)

    def weigh(stored):
        def body(q, carry):
            sums, stress = carry
            values = wave_parts(first_chunk + q)
            gx, gy, gz, inverse = values[3], values[4], values[5], values[7]
            row = lax.div(q, 4) * 8 + lax.rem(q, 4)
            selected = heard[0, pl.ds(row, 1), :] + heard[0, pl.ds(row + 4, 1), :]
            weighted = selected * (4.0 * math.pi) * inverse
            reduced = 2.0 * weighted * inverse
            terms = (
                weighted, reduced * gx * gx, reduced * gy * gy, reduced * gz * gz,
                reduced * gx * gy, reduced * gx * gz, reduced * gy * gz,
            )
            stress = tuple(a + b for a, b in zip(stress, terms))
            for b in range(count_atoms // stride):
                where = pl.ds(b * stride, stride)
                wave = waves[q, where] if stored else wave_block(values, b)
                sums[where] = sums[where] + weighted * wave
            return sums, stress

        return body

    def weigh_all(stored, low, high, stress, sums):
        def body(q, stress):
            return weigh(stored)(q, (sums, stress))[1]

        return lax.fori_loop(low, high, body, stress)

    sums[...] = jnp.zeros((count_atoms, LANES), F32)
    stress = weigh_all(True, 0, kept, (zero,) * 7, sums)
    if kept < share:
        stress = weigh_all(False, kept, share, stress, sums)
    blocks = []
    for b in range(count_atoms // LANES):
        blocks.append(jnp.sum(sums[pl.ds(b * LANES, LANES)].T, axis=0, keepdims=True))
    ballot = jnp.concatenate(blocks + list(stress), axis=0)
    out[...] = jnp.zeros_like(out)
    out[pl.ds(0, ballot.shape[0])] = ballot

    def vote(step):
        return remote(
            out, votes.at[me], vote_send.at[step - 1], vote_recv.at[step - 1],
            at(lax.rem(me + step, everyone)),
        )

    def cast(step, carry):
        vote(step).start()
        return carry

    def count_votes(step, carry):
        vote(step).wait_recv()
        return carry

    def settle(step, carry):
        vote(step).wait_send()
        return carry

    lax.fori_loop(1, everyone, cast, 0)
    votes[me] = out[...]

    for c in range(CUTS):
        to_side(c).wait_send()
        to_mate(c).wait_send()
        mate_side(c).wait_send()

        @pl.when(leads)
        def _():
            to_far(c).wait_send()
            hand_on(c).wait_send()
            mate_far(c).wait_send()
            mate_hand(c).wait_send()

    @pl.when(lists_here)
    def _():
        def sent(step, carry):
            list_copy(my_slot, step).wait_send()
            return carry

        lax.fori_loop(1, grids, sent, 0)

    for batch in range(2):
        def drain(j, carry):
            for upward in (True, False):
                @pl.when(jnp.logical_not(ends(upward)))
                def _():
                    hop(batch, upward, j, boxes[batch])[1].wait_send()
            return carry

        lax.fori_loop(0, pieces, drain, 0)

    @pl.when(owner)
    def _():
        def finish(index, carry):
            @pl.when(index + offset != order)
            def _():
                deliver(index).wait_send()
            return carry

        lax.fori_loop(0, near, finish, 0)

    lax.fori_loop(1, everyone, count_votes, 0)
    lax.fori_loop(1, everyone, settle, 0)
    result = votes[0]
    result = lax.fori_loop(1, everyone, lambda i, total: total + votes[i], result)
    out[...] = result


def exchange(own, listing, atoms, tables, turns, size_x, slabs, items):
    bands, grids = lax.axis_size("band"), lax.axis_size("grid")
    links, everyone = grids // 2, bands * grids
    pair, slab_x, size_y, size_z = own.shape
    groups = slabs * items // 4
    pieces = math.gcd(groups // 2, 12)
    near = 2 * (bands // 2) * links // 2
    share = slabs * items // 2 // near
    assert share % 4 == 0 and groups % 2 == 0
    counts = [len(b) for b in BATCHES]
    kept_rows = size_y // 4 + 1
    count_atoms = atoms.shape[1]
    mib = 1024 * 1024
    used = 4 * LANES * (
        6 * pair * slab_x * size_y + kept_rows * sum(counts) * 4 * DEPTH + 2 * groups * 8 * sum(counts)
        + slabs * (items + 8) + groups * 4 + 4 * share * 2 + everyone * 16
        + pair * slab_x * size_y + 4 * count_atoms + 4000
    )
    kept = max(0, min(share, (VMEM_LIMIT - 3 * mib - used) // (4 * LANES * count_atoms)))
    plan = (size_x, slabs, items, pieces, share, kept)
    vmem = pl.BlockSpec(memory_space=pltpu.VMEM)
    dma = lambda n: pltpu.SemaphoreType.DMA((n,))
    cut = lambda: dma(CUTS)
    ins = [own, listing, atoms, *tables, turns]
    return pl.pallas_call(
        functools.partial(exchange_kernel, plan),
        out_shape=jax.ShapeDtypeStruct((16, LANES), F32),
        in_specs=[vmem] * len(ins),
        out_specs=vmem,
        scratch_shapes=[
            pltpu.VMEM((6 * pair, slab_x, size_y, size_z), F32),
            *[pltpu.VMEM((kept_rows, n * 4 * DEPTH, size_z), F32) for n in counts],
            *[pltpu.VMEM((groups * 8 * n, LANES), F32) for n in counts],
            *[pltpu.VMEM((groups * 8 * n, LANES), F32) for n in counts],
            pltpu.VMEM((slabs * (items + 8), LANES), jnp.int32),
            pltpu.SMEM((slabs * 8, LANES), jnp.int32),
            pltpu.VMEM((groups // 2 * 8, LANES), F32),
            pltpu.VMEM((2 * (bands // 2), share * 2, LANES), F32),
            pltpu.VMEM((everyone, 16, LANES), F32),
            pltpu.VMEM((max(kept, 1), count_atoms, LANES), F32),
            pltpu.VMEM((count_atoms, LANES), F32),
            dma(grids - 1), dma(slabs), dma(slabs),
            cut(), cut(), cut(), cut(), cut(), cut(), cut(), cut(),
            cut(), cut(), cut(), cut(), cut(), cut(), dma(2),
            dma(4 * pieces), dma(4 * pieces),
            dma(near), dma(2 * (bands // 2)),
            dma(everyone - 1), dma(everyone - 1),
        ],
        compiler_params=pltpu.CompilerParams(
            collective_id=0, has_side_effects=True, vmem_limit_bytes=VMEM_LIMIT
        ),
        name="exchange",
    )(*ins)


def per_device(orbitals, occupation, g_list, positions, species, widths):
    bands, slab_x, size_y, size_z = orbitals.shape
    grids, groups = lax.axis_size("grid"), lax.axis_size("band")
    size_x = slab_x * grids
    slab_y = size_y // grids
    assert bands == 2 and groups == 4 and grids % 4 == 0 and size_z == LANES and size_x == LANES
    grid, band = lax.axis_index("grid"), lax.axis_index("band")
    core, mate = band % 2, grid % 2

    plane = size_x * size_z
    key = g_list // size_z % slab_y * plane + g_list // (slab_y * size_z) * size_z + g_list % size_z
    key = lax.sort(key)
    upper = grid >= grids // 2
    x_of, z_of = key // size_z % size_x, key % size_z
    x_of = jnp.where(upper, (size_x - x_of) % size_x, x_of)
    z_of = jnp.where(upper, (size_z - z_of) % size_z, z_of)
    codes = (x_of * size_z + z_of).astype(jnp.int32).reshape(-1, LANES)
    codes = jnp.pad(codes, ((0, 8), (0, 0)))
    ends = jnp.sum((key[None, :] < (jnp.arange(slab_y)[:, None] + 1) * plane).astype(jnp.int32), axis=1)
    middle = ((grid >= grids // 4) & (grid < 3 * grids // 4)).astype(jnp.int32)
    first = jnp.where(upper, size_y - grid * slab_y, grid * slab_y) - middle * (size_y // 4)
    at = jnp.stack([first, jnp.where(upper, -1, 1)]).astype(jnp.int32)
    items = g_list.shape[0] // LANES + -(-slab_y // 16) * 16
    listing = pad_planes(codes, ends.astype(jnp.int32), at, items)

    own = orbitals * jnp.sqrt(occupation)[:, None, None, None]
    width = widths[species]
    atoms = jnp.concatenate([positions, (-0.5 * width * width)[None, :]], axis=0)
    atoms = jnp.broadcast_to(atoms[:, :, None], atoms.shape + (LANES,))
    tables = constant_tables(slab_x, grids, size_y, size_z)
    pick = lambda table, index: lax.dynamic_index_in_dim(jnp.asarray(table), index, 0, keepdims=False)
    held = (pick(tables[0], core), pick(tables[1], core), jnp.asarray(tables[2]), jnp.asarray(tables[3]))
    turns = jnp.stack([pick(tables[4], grid), pick(tables[4], grid + 1 - 2 * mate)])

    out = exchange(own, listing, atoms, held, turns, size_x, grids // 2, items) / float(bands * groups)
    count = positions.shape[1]
    rows = count // LANES
    total, xx, yy, zz, xy, xz, yz = [jnp.sum(out[rows + i]) for i in range(7)]
    stress = jnp.stack([xx - total, xy, xz, xy, yy - total, yz, xz, yz, zz - total]).reshape(3, 3)
    return stress, out[:rows].reshape(-1)


def solution(mesh):
    return jax.shard_map(
        per_device,
        mesh=mesh,
        in_specs=(P("band", "grid", None, None), P("band"), P("grid"), P(), P(), P()),
        out_specs=(P(), P()),
        check_vma=False,
    )
```

profile of v0, /device:TPU:0, one launch (start us, length us, event | category | flops | bytes accessed | tf_op | source)
XLA Modules:
  0.0 245.1 jit_solution(7426828414335985490)
XLA Ops:
  0.6 0.0 copy-start
  0.7 0.6 pad_add_fusion.at
  1.3 0.7 sqrt.3
  1.9 1.5 fusion.21
  3.4 3.2 %select_select_fusion = f32[512]{0:T(512)S(1)} fusion(s32[512]{0:T(512)} %param.15, f32[]{:T(128)} %bitcast.3, f32[]{:T(128)} %bitcast.4, f32[]{:T(128)} %bitcast.5, f32[]{:T(128)} %bitcast.6), kind=kLoop, calls=%fused_computation.58 | loop fusion | flops 4608 | bytes 4112 | tf_op jit(solution)/shard_map/gather | solution.py:724
  6.7 0.7 pad_maximum_fusion.1
  7.4 1.3 dynamic-slice_bitcast_fusion.1.basis_low
  8.7 0.7 constant_dynamic-slice_fusion.1
  9.4 0.6 pad_maximum_fusion.turns
  10.0 1.4 dynamic-slice_bitcast_fusion.basis_wide
  11.4 1.0 fusion.3
  12.4 7.7 %sort.14 = (s32[16384]{0:T(1024)S(1)}, s32[16384]{0:T(1024)}) sort(s32[16384]{0:T(1024)S(1)} %fusion.3, s32[16384]{0:T(1024)S(1)} %iota.8), dimensions={0}, to_apply=%region_0.1 | sort | flops 229376 | bytes 262144 | tf_op jit(solution)/shard_map/sort | solution.py:709
  20.1 0.9 convert_reduce_fusion.ends
  21.0 0.1 fusion.11
  21.1 0.6 pad.4.codes
  21.8 13.8 %pad_planes.1.listing = s32[152,128]{1,0:T(8,128)} custom-call(s32[16]{0:T(128)} %convert_reduce_fusion.ends, s32[2]{0:T(128)} %pad_add_fusion.at, s32[136,128]{1,0:T(8,128)} %pad.4.codes), custom_call_target="tpu_custom_call" | custom-call | tf_op jit(solution)/shard_map/pad_planes/pallas_call | solution.py:120
  35.5 1.3 broadcast_in_dim.5.atoms
  36.8 0.0 copy-done
  36.8 1.7 broadcast_multiply_fusion.own
  38.5 196.4 %exchange.1 = f32[16,128]{1,0:T(8,128)} custom-call(f32[2,16,128,128]{3,2,1,0:T(8,128)} %broadcast_multiply_fusion.own, s32[152,128]{1,0:T(8,128)} %pad_planes.1.listing, f32[4,512,128]{2,1,0:T(8,128)} %broadcast_in_dim.5.atoms, bf16[80,256]{1,0:T(8,128)(2,1)} %dynamic-slice_bitcast_fusion.basis_wide, bf16[80,128]{1,0:T(8,128)(2,1)} %dynamic-slice_bitcast_fusion.1.basis_low, ...), custom_call_target="tpu_custom_call" | custom-call | tf_op jit(solution)/shard_map/exchange/pallas_call | solution.py:667
  234.9 0.7 broadcast_multiply_fusion.1
  235.6 0.6 slice_bitcast_fusion
  236.1 0.7 slice_reduce_fusion
  240.4 4.0 %stack.48 = f32[9]{0:T(128)S(1)} concatenate(f32[1]{0:T(128)} %bitcast.10, f32[1]{0:T(128)} %bitcast.11, f32[1]{0:T(128)} %bitcast.12, f32[1]{0:T(128)} %bitcast.11, f32[1]{0:T(128)} %bitcast.13, f32[1]{0:T(128)} %bitcast.14, f32[1]{0:T(128)} %bitcast.12, f32[1]{0:T(128)} %bitcast.14, f32[1]{0:T(128)} %bitcast.15), dimensions={0} | concatenate | bytes 72 | tf_op jit(solution)/shard_map/stack | solution.py:736
  244.4 0.7 reshape.34
  (3 shorter events, 0.0 us)
Async XLA Ops:
  0.6 36.2 %copy-start = (f32[2,16,128,128]{3,2,1,0:T(8,128)S(1)}, f32[2,16,128,128]{3,2,1,0:T(8,128)}, u32[]{:S(2)}) copy-start(f32[2,16,128,128]{3,2,1,0:T(8,128)} %param.11) | copy-start | bytes 6291460
where the time goes:
time: 246 us; the launch traced here: 245 us
  Pallas kernels  210 us (85%)
  other arithmetic  17.9 us (7%)
  local copies, waits for them, and re-layouts  12.8 us (5%)
  between operations  4.3 us (2%)
    pallas_call x1, Pallas kernels, exchange(): pl.pallas_call(functools.partial(exchange_kernel, plan), out_shape=jax.Sh...  196 us
    pallas_call x1, Pallas kernels, pad_planes(): pl.pallas_call(functools.partial(pad_kernel, ends.shape[0], items), out_s...  13.8 us
    sort x1, other arithmetic, per_device(): key = lax.sort(key)  7.74 us

commit v1 on v0

--- a/solution.py
+++ b/solution.py
@@ -16,6 +16,7 @@
 BF16 = jnp.bfloat16
 LANES = 128
 DEPTH = 8
+RUN = 3
 HOP_LAG = 4
 CUTS = 4
 VMEM_LIMIT = 63 * 1024 * 1024
@@ -88,52 +89,72 @@
     return u * value
 
 
-def pad_kernel(planes, items, ends, at, codes, out):
-    out[...] = jnp.full_like(out, -1)
+def pad_kernel(planes, items, size_y, ends, codes, out, origin, limit, plane_of):
+    grid, grids = lax.axis_index("grid"), lax.axis_size("grid")
+    upper = grid >= grids // 2
+    middle = jnp.logical_and(grid >= grids // 4, grid < 3 * grids // 4)
+    first = jnp.where(upper, size_y - grid * planes, grid * planes) - jnp.where(middle, size_y // 4, 0)
+    sign = jnp.where(upper, -1, 1)
     lane = lax.broadcasted_iota(jnp.int32, (1, LANES), 1)
     flat = lax.broadcasted_iota(jnp.int32, (8, LANES), 0) * LANES + lax.broadcasted_iota(jnp.int32, (8, LANES), 1)
 
-    def one_plane(k, carry):
+    def one_plane(k, place):
         start = jnp.where(k == 0, 0, ends[jnp.maximum(k - 1, 0)])
         end = ends[k]
+
+        def one_row(c, carry):
+            origin[place + c] = start + c * LANES
+            limit[place + c] = end
+            plane_of[place + c] = first + sign * k
+            return carry
+
         count = lax.div(end - start + LANES - 1, LANES)
-
-        def one_row(c, carry):
-            place, marks = carry
-            source = start + c * LANES
-            row, shift = lax.div(source, LANES), lax.rem(source, LANES)
-            index = jnp.broadcast_to(lax.rem(lane + shift, LANES), (8, LANES))
+        lax.fori_loop(0, count, one_row, 0)
+        return place + count
+
+    used = lax.fori_loop(0, planes, one_plane, 0)
+
+    def unused(i, carry):
+        origin[i] = 0
+        limit[i] = 0
+        plane_of[i] = 0
+        return carry
+
+    lax.fori_loop(used, items, unused, 0)
+    steps = 16
+
+    def some_rows(i, marks):
+        for u in range(steps):
+            place = i * steps + u
+            source = origin[place]
+            row, shift = lax.shift_right_logical(source, 7), source & (LANES - 1)
+            index = jnp.broadcast_to((lane + shift) & (LANES - 1), (8, LANES))
             pick = lambda r: jnp.take_along_axis(
-                jnp.broadcast_to(codes[pl.ds(r, 1), :], (8, LANES)), index, axis=1
+                jnp.broadcast_to(codes[pl.ds(r, 1), :], (8, LANES)), index, axis=1, mode="promise_in_bounds"
             )[0:1]
             value = jnp.where(lane + shift < LANES, pick(row), pick(row + 1))
-            out[pl.ds(place, 1), :] = jnp.where(source + lane < end, value, -1)
-            return place + 1, jnp.where(flat == place, at[0] + at[1] * k, marks)
-
-        return lax.fori_loop(0, count, one_row, carry)
-
-    marks = lax.fori_loop(0, planes, one_plane, (0, jnp.zeros((8, LANES), jnp.int32)))[1]
-    out[pl.ds(items, 8), :] = marks
-
-
-def pad_planes(codes, ends, at, items):
+            out[pl.ds(place, 1), :] = jnp.where(source + lane < limit[place], value, -1)
+            marks = jnp.where(flat == place, plane_of[place], marks)
+        return marks
+
+    out[pl.ds(items, 8), :] = lax.fori_loop(0, items // steps, some_rows, jnp.zeros((8, LANES), jnp.int32))
+
+
+def pad_planes(codes, ends, size_y, items):
     return pl.pallas_call(
-        functools.partial(pad_kernel, ends.shape[0], items),
+        functools.partial(pad_kernel, ends.shape[0], items, size_y),
         out_shape=jax.ShapeDtypeStruct((items + 8, LANES), jnp.int32),
-        grid_spec=pltpu.PrefetchScalarGridSpec(
-            num_scalar_prefetch=2,
-            grid=(1,),
-            in_specs=[pl.BlockSpec(codes.shape, lambda i, *_: (0, 0))],
-            out_specs=pl.BlockSpec((items + 8, LANES), lambda i, *_: (0, 0)),
-        ),
+        in_specs=[pl.BlockSpec(memory_space=pltpu.SMEM), pl.BlockSpec(memory_space=pltpu.VMEM)],
+        out_specs=pl.BlockSpec(memory_space=pltpu.VMEM),
+        scratch_shapes=[pltpu.SMEM((items,), jnp.int32)] * 3,
         name="pad_planes",
-    )(ends, at, codes)
+    )(ends, codes)
 
 
 def exchange_kernel(
     plan,
-    own, listing, atoms, basis_wide, basis_low, table_wide, table_low, turns, out,
-    store, planes_a, planes_b, part_a, part_b, box_a, box_b, lists, marks, power, heard, votes, waves, sums,
+    occupation, widths, own, listing, positions, species, basis_wide, basis_low, table_wide, table_low, turns, out,
+    store, planes_a, planes_b, part_a, part_b, box_a, box_b, lists, marks, power, heard, votes, waves, sums, atoms,
     list_send, list_recv, mark_sem, side_send, side_recv, mate_send, mate_recv, lane_send, lane_recv,
     far_send, far_recv, hand_send, hand_recv, away_send, away_recv, pass_send, pass_recv, copy_sem,
     hop_send, hop_recv, share_send, share_recv, vote_send, vote_recv,
@@ -149,9 +170,10 @@
     slab_x, size_y, size_z = own.shape[1:]
     planes, parts, boxes = (planes_a, planes_b), (part_a, part_b), (box_a, box_b)
     leads = core == mate
+    grid_of = (grid, grid + 1 - 2 * mate)
     quarter = grids // 4
     height = items + 8
-    rows = basis_low.shape[0] // 2
+    rows = basis_low.shape[1] // 2
     kept_rows = size_y // 4 + 1
 
     def at(index):
@@ -164,6 +186,14 @@
         return carry
 
     lax.fori_loop(1, everyone, greet, 0)
+    for i in range(own.shape[0]):
+        scale = jnp.sqrt(jnp.full((size_y, size_z), occupation[i], F32))
+
+        def scale_plane(j, carry):
+            store[i, j] = own[i, j] * scale
+            return carry
+
+        lax.fori_loop(0, slab_x, scale_plane, 0)
     pl.semaphore_wait(barrier, everyone - 1)
 
     def remote(source, target, send, recv, device):
@@ -188,7 +218,7 @@
         )
 
     own_list = pltpu.make_async_copy(
-        listing, lists.at[pl.ds(pl.multiple_of(my_slot * height, 8), height)], copy_sem.at[1]
+        listing, lists.at[pl.ds(pl.multiple_of(my_slot * height, 8), height)], copy_sem.at[0]
     )
 
     @pl.when(lists_here)
@@ -202,7 +232,7 @@
 
     cut = slab_x // (CUTS // 2)
     place = lambda group, slab, c: store.at[(group * 2 + slab) * 2 + c % 2, pl.ds(c // 2 * cut, cut)]
-    mine = lambda c: own.at[c % 2, pl.ds(c // 2 * cut, cut)]
+    mine = lambda c: place(0, 0, c)
     to_side = lambda c: remote(mine(c), place(1, 0, c), side_send.at[c], side_recv.at[c], beside)
     to_mate = lambda c: remote(mine(c), place(0, 1, c), mate_send.at[c], mate_recv.at[c], across)
     to_far = lambda c: remote(mine(c), place(2, 0, c), far_send.at[c], far_recv.at[c], far)
@@ -210,8 +240,6 @@
     mate_side = lambda c: remote(place(0, 1, c), place(1, 1, c), lane_send.at[c], lane_recv.at[c], beside)
     mate_far = lambda c: remote(place(0, 1, c), place(2, 1, c), away_send.at[c], away_recv.at[c], far)
     mate_hand = lambda c: remote(place(2, 1, c), place(2, 1, c), pass_send.at[c], pass_recv.at[c], beside)
-    keep = pltpu.make_async_copy(own, store.at[pl.ds(0, 2)], copy_sem.at[0])
-    keep.start()
     for c in range(CUTS):
         to_side(c).start()
         to_mate(c).start()
@@ -271,8 +299,8 @@
                     below = store[left, down] * store[right, down]
                     stack += [above + below, above - below]
                 high, low = split(jnp.concatenate(stack, axis=1))
-                along = dot(basis_wide[...], jnp.concatenate([high, low], axis=0))
-                along = along + dot(basis_low[...], high)
+                along = dot(basis_wide[core], jnp.concatenate([high, low], axis=0))
+                along = along + dot(basis_low[core], high)
                 stack = [along[:, i * size_z : (i + 1) * size_z] for i in range(2 * unroll)]
                 high, low = split(jnp.concatenate(stack, axis=0))
                 both = dot(jnp.concatenate([high, low], axis=1), table_wide[...])
@@ -294,26 +322,39 @@
         slot, r = lax.div(t, items), lax.rem(t, items)
         return slot, r, lists[pl.ds(slot * height + r, 1), :]
 
-    def select(batch, slab, group):
+    def mark(slot, r):
+        return marks[slot * 8 + lax.shift_right_logical(r, 7), r & (LANES - 1)]
+
+    def select(batch, slab, step):
         pairs, source, part = BATCHES[batch], planes[batch], parts[batch]
         count = len(pairs)
-        for u in range(4):
-            slot, r, code = code_row(group * 4 + u)
-            k = marks[slot * 8 + lax.div(r, LANES), lax.rem(r, LANES)]
-            x_of = jnp.broadcast_to(lax.shift_right_arithmetic(code, size_z.bit_length() - 1) & (size_x - 1), (8, LANES))
+        first = step * (4 * RUN)
+        slot = lax.div(first, items)
+        r = lax.rem(first, items)
+        top = slot * height + r
+        base = pl.multiple_of(step * (RUN * 8 * count), 8)
+        for t in range(4 * RUN):
+            code = lists[pl.ds(top + t, 1), :]
+            k = mark(slot, r + t)
+            x_of = lax.shift_right_logical(code, size_z.bit_length() - 1) & (size_x - 1)
+            x_of = jnp.broadcast_to(x_of, (8, LANES))
             z_of = jnp.broadcast_to(code & (size_z - 1), (8, LANES))
-            turn = lambda i: jnp.take_along_axis(turns[slab, pl.ds(8 * i, 8), :], x_of, axis=1)
+            turn = lambda i: jnp.take_along_axis(
+                turns[grid_of[slab], pl.ds(8 * i, 8), :], x_of, axis=1, mode="promise_in_bounds"
+            )
+            get = lambda i: jnp.take_along_axis(
+                source[k, pl.ds(8 * i, 8), :], z_of, axis=1, mode="promise_in_bounds"
+            )
             cosine, sine, phase = turn(0), turn(1), turn(2)
             phase_cos, phase_sin = phase[0:1], phase[1:2]
             for p in range(count):
-                get = lambda i: jnp.take_along_axis(source[k, pl.ds((p * 4 + i) * 8, 8), :], z_of, axis=1)
-                real = jnp.sum(get(0) * cosine + get(3) * sine, axis=0, keepdims=True)
-                imag = jnp.sum(get(1) * cosine - get(2) * sine, axis=0, keepdims=True)
+                real = jnp.sum(get(4 * p) * cosine + get(4 * p + 3) * sine, axis=0, keepdims=True)
+                imag = jnp.sum(get(4 * p + 1) * cosine - get(4 * p + 2) * sine, axis=0, keepdims=True)
                 for which, value in (
                     (0, real * phase_cos + imag * phase_sin),
                     (4, imag * phase_cos - real * phase_sin),
                 ):
-                    row = pl.ds(group * (8 * count) + p * 8 + which + u, 1)
+                    row = pl.ds(base + (t // 4 * 8 * count + p * 8 + which + t % 4), 1)
                     part[row, :] = value if slab == 0 else part[row, :] + value
 
     groups = slabs * items // 4
@@ -366,7 +407,7 @@
 
     def wave_parts(t):
         slot, r, code = code_row(t)
-        k = marks[slot * 8 + lax.div(r, LANES), lax.rem(r, LANES)]
+        k = mark(slot, r)
         valid = code >= 0
         x_of = lax.shift_right_arithmetic(code, size_z.bit_length() - 1) & (size_x - 1)
         z_of = code & (size_z - 1)
@@ -399,7 +440,15 @@
 
     for c in range(CUTS):
         to_side(c).wait_recv()
-    keep.wait()
+    for b in range(count_atoms // LANES):
+        lanes_at = pl.ds(b * LANES, LANES)
+        kind = species[pl.ds(b, 1), :]
+        square = jnp.zeros((1, LANES), F32)
+        for i in range(widths.shape[0]):
+            square = jnp.where(kind == i, -0.5 * widths[i] * widths[i], square)
+        lines = [positions[pl.ds(i, 1), lanes_at] for i in range(3)] + [square]
+        for i, line in enumerate(lines):
+            atoms[i, lanes_at] = jnp.broadcast_to(line, (LANES, LANES)).T
     transform(0, 0)
 
     for slot in range(slabs):
@@ -425,13 +474,13 @@
         mark_copy(slot).wait()
 
     def select_run(batch, slab, low, high):
-        def body(group, carry):
-            select(batch, slab, group)
+        def body(step, carry):
+            select(batch, slab, step)
             return carry
 
         lax.fori_loop(low, high, body, 0)
 
-    spans = [groups * i // CUTS for i in range(CUTS + 1)]
+    spans = [groups // RUN * i // CUTS for i in range(CUTS + 1)]
     for c in range(CUTS):
         relay_far(c)
         select_run(0, 0, spans[c], spans[c + 1])
@@ -454,17 +503,32 @@
         mate_side(c).wait_recv()
     transform(0, 1)
 
+    def keep_wave(q):
+        values = wave_parts(first_chunk + q)
+        for b in range(count_atoms // stride):
+            waves[q, pl.ds(b * stride, stride)] = wave_block(values, b)
+
+    each = -(-kept // pieces)
+
+    def keep_waves(i):
+        for w in range(each):
+            @pl.when(i * each + w < kept)
+            def _():
+                keep_wave(i * each + w)
+
     def one_piece(batch):
         def body(i, carry):
             for upward in (True, False):
-                base = (i + (pieces if upward else 0)) * piece
-                select_run(batch, 1, base, base + piece)
+                base = (i + (pieces if upward else 0)) * (piece // RUN)
+                select_run(batch, 1, base, base + piece // RUN)
 
                 @pl.when(begins(upward))
                 def _():
                     hop(batch, upward, i, parts[batch])[1].start()
 
             chain_step(i + batch * pieces)
+            if batch == 1:
+                keep_waves(i)
             return carry
 
         return body
@@ -479,18 +543,11 @@
     transform(1, 1)
     lax.fori_loop(0, pieces, one_piece(1), 0)
 
-    def keep_wave(q, carry):
-        values = wave_parts(first_chunk + q)
-        for b in range(count_atoms // stride):
-            waves[q, pl.ds(b * stride, stride)] = wave_block(values, b)
-        return carry
-
     def run_out(step, carry):
         chain_step(step)
         return carry
 
     last = 2 * pieces
-    lax.fori_loop(0, kept, keep_wave, 0)
     lax.fori_loop(last, last + HOP_LAG * (links - 1), run_out, 0)
 
     owner = jnp.logical_or(link == 0, link == links - 1)
@@ -637,10 +694,19 @@
     lax.fori_loop(1, everyone, settle, 0)
     result = votes[0]
     result = lax.fori_loop(1, everyone, lambda i, total: total + votes[i], result)
+    result = result * (1.0 / (own.shape[0] * bands))
+    first_row = count_atoms // LANES
+    lines = jnp.sum(result, axis=1, keepdims=True)
+    total, xx, yy, zz, xy, xz, yz = [lines[first_row + i : first_row + i + 1] for i in range(7)]
+    lane = lax.broadcasted_iota(jnp.int32, (1, LANES), 1)
+    row = jnp.zeros((1, LANES), F32)
+    for i, value in enumerate((xx - total, xy, xz, xy, yy - total, yz, xz, yz, zz - total)):
+        row = jnp.where(lane == i, value, row)
     out[...] = result
-
-
-def exchange(own, listing, atoms, tables, turns, size_x, slabs, items):
+    out[pl.ds(first_row, 1)] = row
+
+
+def exchange(own, occupation, listing, positions, species, widths, tables, turns, size_x, slabs, items):
     bands, grids = lax.axis_size("band"), lax.axis_size("grid")
     links, everyone = grids // 2, bands * grids
     pair, slab_x, size_y, size_z = own.shape
@@ -649,25 +715,27 @@
     near = 2 * (bands // 2) * links // 2
     share = slabs * items // 2 // near
     assert share % 4 == 0 and groups % 2 == 0
+    assert groups // 2 // pieces % RUN == 0 and items % (4 * RUN) == 0
     counts = [len(b) for b in BATCHES]
     kept_rows = size_y // 4 + 1
-    count_atoms = atoms.shape[1]
+    count_atoms = positions.shape[1]
     mib = 1024 * 1024
     used = 4 * LANES * (
         6 * pair * slab_x * size_y + kept_rows * sum(counts) * 4 * DEPTH + 2 * groups * 8 * sum(counts)
         + slabs * (items + 8) + groups * 4 + 4 * share * 2 + everyone * 16
-        + pair * slab_x * size_y + 4 * count_atoms + 4000
+        + pair * slab_x * size_y + 5 * count_atoms + 4000
     )
     kept = max(0, min(share, (VMEM_LIMIT - 3 * mib - used) // (4 * LANES * count_atoms)))
     plan = (size_x, slabs, items, pieces, share, kept)
     vmem = pl.BlockSpec(memory_space=pltpu.VMEM)
     dma = lambda n: pltpu.SemaphoreType.DMA((n,))
     cut = lambda: dma(CUTS)
-    ins = [own, listing, atoms, *tables, turns]
+    ins = [occupation, widths, own, listing, positions, species.reshape(-1, LANES), *tables, turns]
+    smem = pl.BlockSpec(memory_space=pltpu.SMEM)
     return pl.pallas_call(
         functools.partial(exchange_kernel, plan),
         out_shape=jax.ShapeDtypeStruct((16, LANES), F32),
-        in_specs=[vmem] * len(ins),
+        in_specs=[smem] * 2 + [vmem] * (len(ins) - 2),
         out_specs=vmem,
         scratch_shapes=[
             pltpu.VMEM((6 * pair, slab_x, size_y, size_z), F32),
@@ -681,9 +749,10 @@
             pltpu.VMEM((everyone, 16, LANES), F32),
             pltpu.VMEM((max(kept, 1), count_atoms, LANES), F32),
             pltpu.VMEM((count_atoms, LANES), F32),
+            pltpu.VMEM((4, count_atoms, LANES), F32),
             dma(grids - 1), dma(slabs), dma(slabs),
             cut(), cut(), cut(), cut(), cut(), cut(), cut(), cut(),
-            cut(), cut(), cut(), cut(), cut(), cut(), dma(2),
+            cut(), cut(), cut(), cut(), cut(), cut(), dma(1),
             dma(4 * pieces), dma(4 * pieces),
             dma(near), dma(2 * (bands // 2)),
             dma(everyone - 1), dma(everyone - 1),
@@ -701,8 +770,7 @@
     size_x = slab_x * grids
     slab_y = size_y // grids
     assert bands == 2 and groups == 4 and grids % 4 == 0 and size_z == LANES and size_x == LANES
-    grid, band = lax.axis_index("grid"), lax.axis_index("band")
-    core, mate = band % 2, grid % 2
+    grid = lax.axis_index("grid")
 
     plane = size_x * size_z
     key = g_list // size_z % slab_y * plane + g_list // (slab_y * size_z) * size_z + g_list % size_z
@@ -714,27 +782,15 @@
     codes = (x_of * size_z + z_of).astype(jnp.int32).reshape(-1, LANES)
     codes = jnp.pad(codes, ((0, 8), (0, 0)))
     ends = jnp.sum((key[None, :] < (jnp.arange(slab_y)[:, None] + 1) * plane).astype(jnp.int32), axis=1)
-    middle = ((grid >= grids // 4) & (grid < 3 * grids // 4)).astype(jnp.int32)
-    first = jnp.where(upper, size_y - grid * slab_y, grid * slab_y) - middle * (size_y // 4)
-    at = jnp.stack([first, jnp.where(upper, -1, 1)]).astype(jnp.int32)
     items = g_list.shape[0] // LANES + -(-slab_y // 16) * 16
-    listing = pad_planes(codes, ends.astype(jnp.int32), at, items)
-
-    own = orbitals * jnp.sqrt(occupation)[:, None, None, None]
-    width = widths[species]
-    atoms = jnp.concatenate([positions, (-0.5 * width * width)[None, :]], axis=0)
-    atoms = jnp.broadcast_to(atoms[:, :, None], atoms.shape + (LANES,))
+    listing = pad_planes(codes, ends.astype(jnp.int32), size_y, items)
+
     tables = constant_tables(slab_x, grids, size_y, size_z)
-    pick = lambda table, index: lax.dynamic_index_in_dim(jnp.asarray(table), index, 0, keepdims=False)
-    held = (pick(tables[0], core), pick(tables[1], core), jnp.asarray(tables[2]), jnp.asarray(tables[3]))
-    turns = jnp.stack([pick(tables[4], grid), pick(tables[4], grid + 1 - 2 * mate)])
-
-    out = exchange(own, listing, atoms, held, turns, size_x, grids // 2, items) / float(bands * groups)
-    count = positions.shape[1]
-    rows = count // LANES
-    total, xx, yy, zz, xy, xz, yz = [jnp.sum(out[rows + i]) for i in range(7)]
-    stress = jnp.stack([xx - total, xy, xz, xy, yy - total, yz, xz, yz, zz - total]).reshape(3, 3)
-    return stress, out[:rows].reshape(-1)
+    *held, turns = [jnp.asarray(table) for table in tables]
+
+    out = exchange(orbitals, occupation, listing, positions, species, widths, held, turns, size_x, grids // 2, items)
+    rows = positions.shape[1] // LANES
+    return out[rows, :9].reshape(3, 3), out[:rows].reshape(-1)
 
 
 def solution(mesh):

time: 246 us -> 190 us (0.77)
  Pallas kernels: 210 us -> 176 us
  local copies, waits for them, and re-layouts: 12.8 us -> 3.25 us
  other arithmetic: 17.9 us -> 9.71 us
  between operations: 4.3 us -> 0.66 us
    pallas_call x1, Pallas kernels: 196 us -> 172 us  [exchange(): pl.pallas_call(functools.partial(exchange_kernel, plan), out_shape=jax.Sh...]
    pallas_call x1, Pallas kernels: 13.8 us -> 4.22 us  [pad_planes(): pl.pallas_call(functools.partial(pad_kernel, ends.shape[0], items, size_y...]
    another operation x2, local copies, waits for them, and re-layouts: 4 us -> 0.67 us  [the longest x1 0.66 us: per_device(): return (out[rows, :9].reshape(3, 3), out[:rows].reshape(-1))]
    gather x1 -> x0, other arithmetic: 3.23 us -> none  [per_device(): width = widths[species]]
    squeeze x2 -> x0, local copies, waits for them, and re-layouts: 2.72 us -> none  [per_device(): lax.dynamic_index_in_dim(jnp.asarray(table), index, 0, keepdims=False)]
where the time goes in v1:
time: 190 us
  Pallas kernels  176 us (93%)
  other arithmetic  9.71 us (5%)
  local copies, waits for them, and re-layouts  3.25 us (2%)
    pallas_call x1, Pallas kernels, exchange(): pl.pallas_call(functools.partial(exchange_kernel, plan), out_shape=jax.Sh...  172 us
    sort x1, other arithmetic, per_device(): key = lax.sort(key)  7.74 us
    pallas_call x1, Pallas kernels, pad_planes(): pl.pallas_call(functools.partial(pad_kernel, ends.shape[0], items, size_y...  4.22 us

profile of v1, /device:TPU:0, one launch (start us, length us, event | category | flops | bytes accessed | tf_op | source)
XLA Modules:
  0.0 189.9 jit_solution(286132155138266060)
XLA Ops:
  0.6 1.0 fusion.3
  1.6 7.7 %sort.14 = (s32[16384]{0:T(1024)S(1)}, s32[16384]{0:T(1024)}) sort(s32[16384]{0:T(1024)S(1)} %fusion.3, s32[16384]{0:T(1024)S(1)} %iota.8), dimensions={0}, to_apply=%region_0.1 | sort | flops 229376 | bytes 262144 | tf_op jit(solution)/shard_map/sort | solution.py:777
  9.4 0.9 convert_reduce_fusion.ends
  10.2 0.1 fusion.11
  10.4 0.6 pad.4.codes
  11.0 4.2 %pad_planes.1.listing = s32[152,128]{1,0:T(8,128)} custom-call(s32[16]{0:T(128)} %convert_reduce_fusion.ends, s32[136,128]{1,0:T(8,128)} %pad.4.codes), custom_call_target="tpu_custom_call" | custom-call | tf_op jit(solution)/shard_map/pad_planes/pallas_call | solution.py:144
  15.2 172.1 %exchange.1 = f32[16,128]{1,0:T(8,128)} custom-call(f32[2]{0:T(128)} %occupation.1, f32[4]{0:T(128)} %widths.1, f32[2,16,128,128]{3,2,1,0:T(8,128)} %own.1, s32[152,128]{1,0:T(8,128)} %pad_planes.1.listing, f32[3,512]{1,0:T(4,128)} %positions.1, s32[4,128]{1,0:T(4,128)} %bitcast.5, bf16[2,80,256]{2,1,0:T(8,128)(2,1)} %constant.99.clone.basis_wide, ...), custom_call_target="tpu_custom_call" | custom-call | tf_op jit(solution)/shard_map/exchange/pallas_call | solution.py:735
  187.3 0.7 slice_reduce_fusion
  188.0 1.3 slice_bitcast_fusion
  189.2 0.7 reshape_squeeze.3
  (2 shorter events, 0.0 us)

commit v2 on v1

--- a/solution.py
+++ b/solution.py
@@ -16,8 +16,8 @@
 BF16 = jnp.bfloat16
 LANES = 128
 DEPTH = 8
-RUN = 3
-HOP_LAG = 4
+RUN = 6
+HOP_LAG = 2
 CUTS = 4
 VMEM_LIMIT = 63 * 1024 * 1024
 
@@ -625,9 +625,14 @@
     blocks = []
     for b in range(count_atoms // LANES):
         blocks.append(jnp.sum(sums[pl.ds(b * LANES, LANES)].T, axis=0, keepdims=True))
-    ballot = jnp.concatenate(blocks + list(stress), axis=0)
+    total, xx, yy, zz, xy, xz, yz = [jnp.sum(line, axis=1, keepdims=True) for line in stress]
+    lane = lax.broadcasted_iota(jnp.int32, (1, LANES), 1)
+    row = zero
+    for i, value in enumerate((xx - total, xy, xz, xy, yy - total, yz, xz, yz, zz - total)):
+        row = jnp.where(lane == i, value, row)
+    ballot = jnp.concatenate(blocks + [row], axis=0)
     out[...] = jnp.zeros_like(out)
-    out[pl.ds(0, ballot.shape[0])] = ballot
+    out[pl.ds(0, ballot.shape[0])] = ballot * (1.0 / (own.shape[0] * bands))
 
     def vote(step):
         return remote(
@@ -694,16 +699,7 @@
     lax.fori_loop(1, everyone, settle, 0)
     result = votes[0]
     result = lax.fori_loop(1, everyone, lambda i, total: total + votes[i], result)
-    result = result * (1.0 / (own.shape[0] * bands))
-    first_row = count_atoms // LANES
-    lines = jnp.sum(result, axis=1, keepdims=True)
-    total, xx, yy, zz, xy, xz, yz = [lines[first_row + i : first_row + i + 1] for i in range(7)]
-    lane = lax.broadcasted_iota(jnp.int32, (1, LANES), 1)
-    row = jnp.zeros((1, LANES), F32)
-    for i, value in enumerate((xx - total, xy, xz, xy, yy - total, yz, xz, yz, zz - total)):
-        row = jnp.where(lane == i, value, row)
     out[...] = result
-    out[pl.ds(first_row, 1)] = row
 
 
 def exchange(own, occupation, listing, positions, species, widths, tables, turns, size_x, slabs, items):
@@ -719,10 +715,11 @@
     counts = [len(b) for b in BATCHES]
     kept_rows = size_y // 4 + 1
     count_atoms = positions.shape[1]
+    height = -(-(count_atoms // LANES + 1) // 8) * 8
     mib = 1024 * 1024
     used = 4 * LANES * (
         6 * pair * slab_x * size_y + kept_rows * sum(counts) * 4 * DEPTH + 2 * groups * 8 * sum(counts)
-        + slabs * (items + 8) + groups * 4 + 4 * share * 2 + everyone * 16
+        + slabs * (items + 8) + groups * 4 + 4 * share * 2 + everyone * height
         + pair * slab_x * size_y + 5 * count_atoms + 4000
     )
     kept = max(0, min(share, (VMEM_LIMIT - 3 * mib - used) // (4 * LANES * count_atoms)))
@@ -734,7 +731,7 @@
     smem = pl.BlockSpec(memory_space=pltpu.SMEM)
     return pl.pallas_call(
         functools.partial(exchange_kernel, plan),
-        out_shape=jax.ShapeDtypeStruct((16, LANES), F32),
+        out_shape=jax.ShapeDtypeStruct((height, LANES), F32),
         in_specs=[smem] * 2 + [vmem] * (len(ins) - 2),
         out_specs=vmem,
         scratch_shapes=[
@@ -746,7 +743,7 @@
             pltpu.SMEM((slabs * 8, LANES), jnp.int32),
             pltpu.VMEM((groups // 2 * 8, LANES), F32),
             pltpu.VMEM((2 * (bands // 2), share * 2, LANES), F32),
-            pltpu.VMEM((everyone, 16, LANES), F32),
+            pltpu.VMEM((everyone, height, LANES), F32),
             pltpu.VMEM((max(kept, 1), count_atoms, LANES), F32),
             pltpu.VMEM((count_atoms, LANES), F32),
             pltpu.VMEM((4, count_atoms, LANES), F32),

time: 190 us -> 183 us (0.963)
  Pallas kernels: 176 us -> 169 us
    pallas_call x1, Pallas kernels: 172 us -> 165 us  [exchange(): pl.pallas_call(functools.partial(exchange_kernel, plan), out_shape=jax.Sh...]
where the time goes in v2:
time: 183 us
  Pallas kernels  169 us (92%)
  other arithmetic  9.71 us (5%)
  local copies, waits for them, and re-layouts  3.25 us (2%)
    pallas_call x1, Pallas kernels, exchange(): pl.pallas_call(functools.partial(exchange_kernel, plan), out_shape=jax.Sh...  165 us
    sort x1, other arithmetic, per_device(): key = lax.sort(key)  7.74 us
    pallas_call x1, Pallas kernels, pad_planes(): pl.pallas_call(functools.partial(pad_kernel, ends.shape[0], items, size_y...  4.22 us

profile of v2, /device:TPU:0, one launch (start us, length us, event | category | flops | bytes accessed | tf_op | source)
XLA Modules:
  0.0 183.0 jit_solution(10385649833627174384)
XLA Ops:
  0.6 1.0 fusion.3
  1.6 7.7 %sort.14 = (s32[16384]{0:T(1024)S(1)}, s32[16384]{0:T(1024)}) sort(s32[16384]{0:T(1024)S(1)} %fusion.3, s32[16384]{0:T(1024)S(1)} %iota.8), dimensions={0}, to_apply=%region_0.1 | sort | flops 229376 | bytes 262144 | tf_op jit(solution)/shard_map/sort | solution.py:774
  9.4 0.9 convert_reduce_fusion.ends
  10.2 0.1 fusion.11
  10.4 0.6 pad.4.codes
  11.0 4.2 %pad_planes.1.listing = s32[152,128]{1,0:T(8,128)} custom-call(s32[16]{0:T(128)} %convert_reduce_fusion.ends, s32[136,128]{1,0:T(8,128)} %pad.4.codes), custom_call_target="tpu_custom_call" | custom-call | tf_op jit(solution)/shard_map/pad_planes/pallas_call | solution.py:144
  15.2 165.1 %exchange.1 = f32[8,128]{1,0:T(8,128)} custom-call(f32[2]{0:T(128)} %occupation.1, f32[4]{0:T(128)} %widths.1, f32[2,16,128,128]{3,2,1,0:T(8,128)} %own.1, s32[152,128]{1,0:T(8,128)} %pad_planes.1.listing, f32[3,512]{1,0:T(4,128)} %positions.1, s32[4,128]{1,0:T(4,128)} %bitcast.5, bf16[2,80,256]{2,1,0:T(8,128)(2,1)} %constant.99.clone.basis_wide, ...), custom_call_target="tpu_custom_call" | custom-call | tf_op jit(solution)/shard_map/exchange/pallas_call | solution.py:732
  180.3 0.7 slice_reduce_fusion
  181.0 1.3 slice_bitcast_fusion
  182.3 0.7 reshape_squeeze.3
  (2 shorter events, 0.0 us)
